TPU v7x, 32 devices: a whole 2x2x4 slice. The times are simulated.
32 devices in a mesh: text: 16 (over z, y, x), query: 2 (over core).
Axes of the slice: x: 2, y: 2, z: 4, core: 2. Of those that a mesh axis runs over, the one named last changes fastest.
Arguments:
- query_embed: bfloat16 [1024, 1024], P(('text', 'query')), may hold values from -6 to 6
- truth_ids: int32 [1024], P(('text', 'query')), may hold values from 0 to 8191
- text_embed: bfloat16 [8192, 1024], P('text'), may hold values from -0.1875 to 0.1875
- text_ids: int32 [8192], P('text'), may hold values from 0 to 8191, each once
Outputs:
- top_scores: float32 [1024, 10], P(('text', 'query'))
- margins: float32 [1024, 3], P(('text', 'query'))
Inputs may be any that keep to these rules, and one draw needn't show every extreme that they name: `text_ids`: every id of 0 to 8191 stands in exactly one row.
All inputs are finite; a program needn't handle non-finite values.
Results may differ from a plain program's by a relative error of at most 0.0003.
Values may be sent and summed in bfloat16 or wider, within the bound.
No kernel may reach another device: no remote copies, remote signals or barrier semaphores. Data moves between devices by JAX's collectives and lax.ppermute only.
A program may use at most 64 MiB of HBM per device.

v0:
```python
import jax
import jax.numpy as jnp
from jax import lax
from jax.sharding import PartitionSpec as P

TOPK = 10


def per_device(query_embed, truth_ids, text_embed, text_ids):
    position = lax.axis_index("text")
    own_rows = query_embed.shape[0]
    gathered = lax.all_gather(query_embed, "text", axis=0, tiled=True)
    wanted = lax.all_gather(truth_ids, "text", axis=0, tiled=True)
    row_count = gathered.shape[0]
    block_rows = min(512, row_count)
    block_count = row_count // block_rows

    def score_block(operand):
        query_slab, wanted_ids = operand
        scores = lax.dot_general(
            query_slab, text_embed, (((1,), (1,)), ((), ())), preferred_element_type=jnp.float32
        )
        leaders = lax.top_k(scores, TOPK)[0]
        truth_part = jnp.sum(
            jnp.where(text_ids[None, :] == wanted_ids[:, None], scores, 0.0), axis=1
        )
        return (leaders, truth_part)

    leaders, truth_part = lax.map(
        score_block,
        (
            gathered.reshape(block_count, block_rows, gathered.shape[1]),
            wanted.reshape(block_count, block_rows),
        ),
    )
    leaders = leaders.reshape(row_count, TOPK)
    truth_part = truth_part.reshape(row_count)
    pooled = lax.all_to_all(leaders, "text", split_axis=0, concat_axis=1, tiled=True)
    chosen = lax.top_k(pooled, TOPK)[0]
    summed = lax.psum(truth_part, "text")
    truth_score = lax.dynamic_slice_in_dim(summed, position * own_rows, own_rows, 0)
    margins = jnp.stack(
        [truth_score - chosen[:, 0], truth_score - chosen[:, 4], truth_score - chosen[:, 9]], axis=1
    )
    return (chosen, margins)


def solution(mesh):
    return jax.shard_map(
        per_device,
        mesh=mesh,
        in_specs=(P(("text", "query"), None), P(("text", "query")), P("text", None), P("text")),
        out_specs=(P(("text", "query"), None), P(("text", "query"), None)),
        check_vma=False,
    )
```

profile of v0, /device:TPU:0, one launch (start us, length us, event | category | flops | bytes accessed | tf_op | source)
XLA Modules:
  0.0 162.6 jit_solution(6516423527075687639)
XLA Ops:
  7.2 0.7 all-gather.2.cloned.1.call-update
  7.9 0.6 copy-done.3
  8.6 0.6 dynamic-slice.2
  9.8 0.6 copy-done.2
  10.5 0.2 dynamic-update-slice
  10.7 16.3 %all-reduce = s32[512]{0:T(512)S(1)} all-reduce(s32[512]{0:T(512)S(1)} %dynamic-update-slice), channel_id=1, replica_groups=mesh['text'=16,'query'=2] {'text'}, use_global_device_ids=true, to_apply=%add | all-reduce | flops 512 | bytes 4096
  27.0 41.6 %all-gather.2.cloned.1.call-done = bf16[512,1024]{1,0:T(8,128)(2,1)} async-done(((bf16[32,1024]{1,0:T(8,128)(2,1)}), bf16[512,1024]{1,0:T(8,128)(2,1)}) %all-gather.2.cloned.1.call-update) | async-done | bytes 1048592 | tf_op jit(solution)/shard_map/all_gather | solution.py:12
  68.6 2.0 %select_reduce_fusion = (f32[512]{0:T(512)S(1)}, f32[512,512]{0,1:T(8,128)S(1)}) fusion(s32[512]{0:T(512)S(1)} %all-reduce, s32[512]{0:T(512)S(1)} %copy-done.1, bf16[512,1024]{1,0:T(8,128)(2,1)} %all-gather.2.cloned.1.call-done, bf16[512,1024]{1,0:T(8,128)(2,1)S(1)} %copy-done), kind=kOutput, calls=%fused_computation | convolution fusion | flops 537656832 | bytes 3151872 | tf_op jit(solution)/shard_map/while/body/eval_jaxpr/dot_general | solution.py:20
  70.6 0.1 iota.6.clone
  70.7 29.4 %top_k.14 = (f32[512,512]{0,1:T(8,128)}, s32[512,512]{0,1:T(8,128)}) sort(f32[512,512]{0,1:T(8,128)S(1)} %get-tuple-element.42, s32[512,512]{0,1:T(8,128)S(1)} %iota.6.clone), dimensions={1}, to_apply=%region_0.1 | sort | flops 4718592 | bytes 4194304 | tf_op jit(solution)/shard_map/while/body/eval_jaxpr/top_k | solution.py:23
  100.0 1.6 copy.16
  101.6 0.2 copy.11
  101.8 0.7 reshape.28
  102.5 4.5 %all-to-all-start = ((f32[16,1,320]{2,1,0:T(1,128)}), f32[16,1,320]{2,1,0:T(1,128)S(1)}, u32[]{:S(2)}, u32[]{:S(2)}) async-start(f32[16,1,320]{2,1,0:T(1,128)} %reshape.28), calls=%async_computation | async-start | bytes 49152 | tf_op jit(solution)/shard_map/all_to_all | solution.py:38
  107.0 42.1 %psum.7 = f32[512]{0:T(512)S(1)} all-reduce(f32[512]{0:T(512)S(1)} %get-tuple-element.41), channel_id=1, replica_groups=mesh['text'=16,'query'=2] {'text'}, use_global_device_ids=true, to_apply=%region_3.4 | all-reduce | flops 512 | bytes 4096 | tf_op jit(solution)/shard_map/psum | solution.py:40
  149.1 0.5 broadcast.12
  149.6 0.7 reduce.6
  150.3 0.1 reshape.29
  150.4 0.1 copy.12
  150.5 3.8 %top_k.20 = (f32[32,160]{1,0:T(8,128)S(1)}, s32[32,160]{1,0:T(8,128)}) sort(f32[32,160]{1,0:T(8,128)S(1)} %copy.12, s32[32,160]{1,0:T(8,128)S(1)} %iota.7), dimensions={1}, to_apply=%region_1.2 | sort | flops 66560 | bytes 81920 | tf_op jit(solution)/shard_map/top_k | solution.py:39
  154.3 0.2 slice_reduce_fusion.2
  154.5 0.7 copy.13
  155.1 0.1 subtract_bitcast_fusion.2
  155.2 0.6 pad_maximum_fusion
  (14 shorter events, 0.1 us)
Async XLA Ops:
  7.2 61.4 %copy-start = (bf16[512,1024]{1,0:T(8,128)(2,1)S(1)}, bf16[512,1024]{1,0:T(8,128)(2,1)}, u32[]{:S(2)}) copy-start(bf16[512,1024]{1,0:T(8,128)(2,1)} %param.6) | copy-start | bytes 3145732
  7.2 61.4 %all-gather.2.cloned.1.call-start = ((), (), s32[]{:S(2)}) async-start(), calls=%async_computation.1 | async-start | bytes 1114112 | tf_op jit(solution)/shard_map/all_gather | solution.py:12
  7.9 0.7 copy-start.3
  9.8 0.7 copy-start.2
  10.7 57.9 %copy-start.1 = (s32[512]{0:T(512)S(1)}, s32[512]{0:T(512)}, u32[]{:S(2)}) copy-start(s32[512]{0:T(512)} %param.7) | copy-start | bytes 6148
  102.5 46.5 %all-to-all-start = ((f32[16,1,320]{2,1,0:T(1,128)}), f32[16,1,320]{2,1,0:T(1,128)S(1)}, u32[]{:S(2)}, u32[]{:S(2)}) async-start(f32[16,1,320]{2,1,0:T(1,128)} %reshape.28), calls=%async_computation | async-start | bytes 49152 | tf_op jit(solution)/shard_map/all_to_all | solution.py:38
Sparse Core Ops, SparseCore 0:
  10.7 57.7 all-gather.1
where the time goes:
time: 163 us
  blocking collectives  58.4 us (36%)
  waiting for transfers between devices  42.3 us (26%)
  other arithmetic  34.5 us (21%)
  between operations  14.8 us (9%)
  local copies, waits for them, and re-layouts  6.15 us (4%)
  starting transfers between devices  4.49 us (3%)
  matrix products  1.98 us (1%)
    psum x1, blocking collectives, per_device(): summed = lax.psum(truth_part, 'text')  42.1 us
    all_gather x1, waiting for transfers between devices, per_device(): gathered = lax.all_gather(query_embed, 'text', axis=0, tiled=True)  41.6 us
    top_k x1, other arithmetic, score_block(): leaders = lax.top_k(scores, TOPK)[0]  29.4 us
    unnamed x1, blocking collectives  16.3 us
    all_to_all x1, starting transfers between devices, per_device(): lax.all_to_all(leaders, 'text', split_axis=0, concat_axis=1, tiled=True)  4.45 us
    top_k x1, other arithmetic, per_device(): chosen = lax.top_k(pooled, TOPK)[0]  3.78 us
    unnamed x14, local copies, waits for them, and re-layouts  3.54 us
  transfers between devices with their start and end apart: 2, of which 1 were waited for; matrix products, arithmetic and copies ran while one was open for 0% of the time, Pallas kernels for 0%

commit v1 on v0

--- a/solution.py
+++ b/solution.py
@@ -6,10 +6,23 @@
 TOPK = 10
 
 
+def watch_yards(message, across):
+    met_up = lax.axis_size(across)
+    t1, z_new = (met_up, lax.axis_index(across))
+    v1, heard = (message, 1)
+    while heard < t1:
+        state_next = lax.ppermute(v1, across, perm=[(d, d ^ heard) for d in range(t1)])
+        block_out = jnp.concatenate([v1, state_next], 0)
+        spare = jnp.concatenate([state_next, v1], 0)
+        v1 = jnp.where(z_new & heard == 0, block_out, spare)
+        heard = 2 * heard
+    return v1
+
+
 def per_device(query_embed, truth_ids, text_embed, text_ids):
     position = lax.axis_index("text")
     own_rows = query_embed.shape[0]
-    gathered = lax.all_gather(query_embed, "text", axis=0, tiled=True)
+    gathered = watch_yards(query_embed, "text")
     wanted = lax.all_gather(truth_ids, "text", axis=0, tiled=True)
     row_count = gathered.shape[0]
     block_rows = min(512, row_count)

time: 163 us -> 132 us (0.81)
  waiting for transfers between devices: 42.3 us -> 9.76 us
  starting transfers between devices: 4.49 us -> 18.1 us
  between operations: 14.8 us -> 1.45 us
    all_gather x1 -> x0, waiting for transfers between devices: 41.6 us -> none  [per_device(): gathered = lax.all_gather(query_embed, 'text', axis=0, tiled=True)]
    ppermute x0 -> x4, starting transfers between devices: none -> 11.3 us  [watch_yards(): lax.ppermute(v1, across, perm=[(d, d ^ heard) for d in range(t1)])]
    ppermute x0 -> x4, waiting for transfers between devices: none -> 9.76 us  [watch_yards(): lax.ppermute(v1, across, perm=[(d, d ^ heard) for d in range(t1)])]
    all_to_all x1, starting transfers between devices: 4.45 us -> 6.8 us  [per_device(): lax.all_to_all(leaders, 'text', split_axis=0, concat_axis=1, tiled=True)]
  transfers between devices with their start and end apart: 2 -> 5, of which waited for: 1 -> 3; matrix products, arithmetic and copies ran while one was open for 0% -> 1% of each run, Pallas kernels for 0% -> 0%
where the time goes in v1:
time: 132 us; the launch traced here: 131 us
  blocking collectives  59.6 us (45%)
  other arithmetic  35.6 us (27%)
  starting transfers between devices  18.1 us (14%)
  waiting for transfers between devices  9.76 us (7%)
  local copies, waits for them, and re-layouts  4.93 us (4%)
  matrix products  1.97 us (1%)
  between operations  1.45 us (1%)
    psum x1, blocking collectives, per_device(): summed = lax.psum(truth_part, 'text')  42.1 us
    top_k x1, other arithmetic, score_block(): leaders = lax.top_k(scores, TOPK)[0]  29.4 us
    unnamed x1, blocking collectives  17.5 us
    ppermute x4, starting transfers between devices, watch_yards(): lax.ppermute(v1, across, perm=[(d, d ^ heard) for d in range(t1)])  11.3 us
    ppermute x4, waiting for transfers between devices, watch_yards(): lax.ppermute(v1, across, perm=[(d, d ^ heard) for d in range(t1)])  9.76 us
    all_to_all x1, starting transfers between devices, per_device(): lax.all_to_all(leaders, 'text', split_axis=0, concat_axis=1, tiled=True)  6.8 us
    top_k x1, other arithmetic, per_device(): chosen = lax.top_k(pooled, TOPK)[0]  3.78 us
  transfers between devices with their start and end apart: 5, of which 3 were waited for; matrix products, arithmetic and copies ran while one was open for 1% of the time, Pallas kernels for 0%

profile of v1, /device:TPU:0, one launch (start us, length us, event | category | flops | bytes accessed | tf_op | source)
XLA Modules:
  0.0 131.5 jit_solution(18005538857997733873)
XLA Ops:
  0.7 3.0 %collective-permute-start = (bf16[32,1024]{1,0:T(8,128)(2,1)}, bf16[32,1024]{1,0:T(8,128)(2,1)S(1)}, u32[]{:S(2)}, u32[]{:S(2)}) collective-permute-start(bf16[32,1024]{1,0:T(8,128)(2,1)} %param.4), channel_id=1, source_target_pairs={{0,2},{2,0},{4,6},{6,4},{8,10},{10,8},{12,14},{14,12},{16,18},{18,... | collective-permute-start | bytes 196616 | tf_op jit(solution)/shard_map/ppermute | solution.py:14
  3.7 2.5 %collective-permute-done = bf16[32,1024]{1,0:T(8,128)(2,1)S(1)} collective-permute-done((bf16[32,1024]{1,0:T(8,128)(2,1)}, bf16[32,1024]{1,0:T(8,128)(2,1)S(1)}, u32[]{:S(2)}, u32[]{:S(2)}) %collective-permute-start) | collective-permute-done | bytes 65568 | tf_op jit(solution)/shard_map/ppermute | solution.py:14
  6.2 0.9 maximum_select_fusion.4
  7.1 2.1 %collective-permute-start.1 = (bf16[64,1024]{1,0:T(8,128)(2,1)S(1)}, bf16[64,1024]{1,0:T(8,128)(2,1)S(1)}, u32[]{:S(2)}, u32[]{:S(2)}) collective-permute-start(bf16[64,1024]{1,0:T(8,128)(2,1)S(1)} %maximum_select_fusion.4), channel_id=1, source_target_pairs={{0,4},{2,6},{4,0},{6,2},{8,12},{10,14},{12,8},{14,10},{16,20},{18,... | collective-permute-start | bytes 393224 | tf_op jit(solution)/shard_map/ppermute | solution.py:14
  9.2 2.9 %collective-permute-done.1 = bf16[64,1024]{1,0:T(8,128)(2,1)S(1)} collective-permute-done((bf16[64,1024]{1,0:T(8,128)(2,1)S(1)}, bf16[64,1024]{1,0:T(8,128)(2,1)S(1)}, u32[]{:S(2)}, u32[]{:S(2)}) %collective-permute-start.1) | collective-permute-done | bytes 131104 | tf_op jit(solution)/shard_map/ppermute | solution.py:14
  12.2 2.1 %collective-permute-start.2 = (bf16[128,1024]{1,0:T(8,128)(2,1)S(1)}, bf16[128,1024]{1,0:T(8,128)(2,1)S(1)}, u32[]{:S(2)}, u32[]{:S(2)}) collective-permute-start(bf16[128,1024]{1,0:T(8,128)(2,1)S(1)} %maximum_select_fusion.3), channel_id=1, source_target_pairs={{0,8},{2,10},{4,12},{6,14},{8,0},{10,2},{12,4},{14,6},{16,24},{18,... | collective-permute-start | bytes 786440 | tf_op jit(solution)/shard_map/ppermute | solution.py:14
  14.4 4.4 %collective-permute-done.2 = bf16[128,1024]{1,0:T(8,128)(2,1)S(1)} collective-permute-done((bf16[128,1024]{1,0:T(8,128)(2,1)S(1)}, bf16[128,1024]{1,0:T(8,128)(2,1)S(1)}, u32[]{:S(2)}, u32[]{:S(2)}) %collective-permute-start.2) | collective-permute-done | bytes 262176 | tf_op jit(solution)/shard_map/ppermute | solution.py:14
  18.9 4.0 %collective-permute-start.3 = (bf16[256,1024]{1,0:T(8,128)(2,1)S(1)}, bf16[256,1024]{1,0:T(8,128)(2,1)}, u32[]{:S(2)}, u32[]{:S(2)}) collective-permute-start(bf16[256,1024]{1,0:T(8,128)(2,1)S(1)} %maximum_select_fusion.2), channel_id=1, source_target_pairs={{0,16},{2,18},{4,20},{6,22},{8,24},{10,26},{12,28},{14,30},{16,0},... | collective-permute-start | bytes 1572872 | tf_op jit(solution)/shard_map/ppermute | solution.py:14
  22.9 0.6 dynamic-slice.2
  24.1 0.2 dynamic-update-slice
  24.4 17.5 %all-reduce = s32[512]{0:T(512)S(1)} all-reduce(s32[512]{0:T(512)S(1)} %dynamic-update-slice), channel_id=1, replica_groups=mesh['text'=16,'query'=2] {'text'}, use_global_device_ids=true, to_apply=%add | all-reduce | flops 512 | bytes 4096
  41.9 2.0 %select_reduce_fusion = (f32[512]{0:T(512)S(1)}, f32[512,512]{0,1:T(8,128)S(1)}) fusion(s32[512]{0:T(512)S(1)} %all-reduce, s32[512]{0:T(512)S(1)} %copy-done.1, bf16[512,1024]{1,0:T(8,128)(2,1)S(1)} %copy-done, bf16[256,1024]{1,0:T(8,128)(2,1)} %collective-permute-done.3, bf16[256,1024]{1,0:T(8,128)(2,1)S(1)} %maximum_select_fusion.2, pred[]{:T(512)S(6)} %eq.32), kind=kOutput, calls=%fused_computation.7 | convolution fusion | flops 542375424 | bytes 3151873 | tf_op jit(solution)/shard_map/while/body/eval_jaxpr/dot_general | solution.py:33
  44.0 29.4 %top_k.14 = (f32[512,512]{0,1:T(8,128)}, s32[512,512]{0,1:T(8,128)}) sort(f32[512,512]{0,1:T(8,128)S(1)} %get-tuple-element.42, s32[512,512]{0,1:T(8,128)S(1)} %iota.6.clone), dimensions={1}, to_apply=%region_0.1 | sort | flops 4718592 | bytes 4194304 | tf_op jit(solution)/shard_map/while/body/eval_jaxpr/top_k | solution.py:36
  73.4 1.6 %copy.16 = f32[512,512]{1,0:T(8,128)S(1)} copy(f32[512,512]{0,1:T(8,128)} %get-tuple-element.33) | data formatting | bytes 2097152 | tf_op jit(solution)/shard_map/while/body/eval_jaxpr/top_k | solution.py:36
  75.0 0.2 copy.11
  75.1 0.7 reshape.28
  75.8 6.8 %all-to-all-start = ((f32[16,1,320]{2,1,0:T(1,128)}), f32[16,1,320]{2,1,0:T(1,128)S(1)}, u32[]{:S(2)}, u32[]{:S(2)}) async-start(f32[16,1,320]{2,1,0:T(1,128)} %reshape.28), calls=%async_computation | async-start | bytes 49152 | tf_op jit(solution)/shard_map/all_to_all | solution.py:51
  82.7 42.1 %psum.7 = f32[512]{0:T(512)S(1)} all-reduce(f32[512]{0:T(512)S(1)} %get-tuple-element.41), channel_id=1, replica_groups=mesh['text'=16,'query'=2] {'text'}, use_global_device_ids=true, to_apply=%region_3.4 | all-reduce | flops 512 | bytes 4096 | tf_op jit(solution)/shard_map/psum | solution.py:53
  124.7 0.5 broadcast.12
  125.3 0.7 reduce.6
  126.2 3.8 %top_k.20 = (f32[32,160]{1,0:T(8,128)S(1)}, s32[32,160]{1,0:T(8,128)}) sort(f32[32,160]{1,0:T(8,128)S(1)} %copy.12, s32[32,160]{1,0:T(8,128)S(1)} %iota.7), dimensions={1}, to_apply=%region_1.2 | sort | flops 66560 | bytes 81920 | tf_op jit(solution)/shard_map/top_k | solution.py:52
  130.0 0.2 slice_reduce_fusion.2
  130.1 0.7 copy.13
  130.9 0.6 pad_maximum_fusion
  (22 shorter events, 0.6 us)
Async XLA Ops:
  0.6 41.3 %copy-start = (bf16[512,1024]{1,0:T(8,128)(2,1)S(1)}, bf16[512,1024]{1,0:T(8,128)(2,1)}, u32[]{:S(2)}) copy-start(bf16[512,1024]{1,0:T(8,128)(2,1)} %param.6) | copy-start | bytes 3145732
  0.6 22.2 %copy-start.3 = (u32[32]{0:T(128)S(1)}, u32[32]{0:T(128)}, u32[]{:S(2)}) copy-start(u32[32]{0:T(128)} %constant.53) | copy-start | bytes 388
  0.7 23.5 %copy-start.2 = (s32[32]{0:T(128)S(1)}, s32[32]{0:T(128)}, u32[]{:S(2)}) copy-start(s32[32]{0:T(128)} %param.5) | copy-start | bytes 388
  0.7 41.3 %copy-start.1 = (s32[512]{0:T(512)S(1)}, s32[512]{0:T(512)}, u32[]{:S(2)}) copy-start(s32[512]{0:T(512)} %param.7) | copy-start | bytes 6148
  0.7 5.5 %collective-permute-start = (bf16[32,1024]{1,0:T(8,128)(2,1)}, bf16[32,1024]{1,0:T(8,128)(2,1)S(1)}, u32[]{:S(2)}, u32[]{:S(2)}) collective-permute-start(bf16[32,1024]{1,0:T(8,128)(2,1)} %param.4), channel_id=1, source_target_pairs={{0,2},{2,0},{4,6},{6,4},{8,10},{10,8},{12,14},{14,12},{16,18},{18,... | collective-permute-start | bytes 196616 | tf_op jit(solution)/shard_map/ppermute | solution.py:14
  7.1 5.1 %collective-permute-start.1 = (bf16[64,1024]{1,0:T(8,128)(2,1)S(1)}, bf16[64,1024]{1,0:T(8,128)(2,1)S(1)}, u32[]{:S(2)}, u32[]{:S(2)}) collective-permute-start(bf16[64,1024]{1,0:T(8,128)(2,1)S(1)} %maximum_select_fusion.4), channel_id=1, source_target_pairs={{0,4},{2,6},{4,0},{6,2},{8,12},{10,14},{12,8},{14,10},{16,20},{18,... | collective-permute-start | bytes 393224 | tf_op jit(solution)/shard_map/ppermute | solution.py:14
  12.2 6.5 %collective-permute-start.2 = (bf16[128,1024]{1,0:T(8,128)(2,1)S(1)}, bf16[128,1024]{1,0:T(8,128)(2,1)S(1)}, u32[]{:S(2)}, u32[]{:S(2)}) collective-permute-start(bf16[128,1024]{1,0:T(8,128)(2,1)S(1)} %maximum_select_fusion.3), channel_id=1, source_target_pairs={{0,8},{2,10},{4,12},{6,14},{8,0},{10,2},{12,4},{14,6},{16,24},{18,... | collective-permute-start | bytes 786440 | tf_op jit(solution)/shard_map/ppermute | solution.py:14
  18.9 23.1 %collective-permute-start.3 = (bf16[256,1024]{1,0:T(8,128)(2,1)S(1)}, bf16[256,1024]{1,0:T(8,128)(2,1)}, u32[]{:S(2)}, u32[]{:S(2)}) collective-permute-start(bf16[256,1024]{1,0:T(8,128)(2,1)S(1)} %maximum_select_fusion.2), channel_id=1, source_target_pairs={{0,16},{2,18},{4,20},{6,22},{8,24},{10,26},{12,28},{14,30},{16,0},... | collective-permute-start | bytes 1572872 | tf_op jit(solution)/shard_map/ppermute | solution.py:14
  75.8 48.9 %all-to-all-start = ((f32[16,1,320]{2,1,0:T(1,128)}), f32[16,1,320]{2,1,0:T(1,128)S(1)}, u32[]{:S(2)}, u32[]{:S(2)}) async-start(f32[16,1,320]{2,1,0:T(1,128)} %reshape.28), calls=%async_computation | async-start | bytes 49152 | tf_op jit(solution)/shard_map/all_to_all | solution.py:51
